TPU v7x, 128 devices: a whole 4x4x4 slice. The times are simulated.
128 devices in a mesh: dp: 1, fsdp: 128 (over z, y, x, core).
Axes of the slice: x: 4, y: 4, z: 4, core: 2. Of those that a mesh axis runs over, the one named last changes fastest.
Arguments:
- latents: bfloat16 [512, 256, 1152], P(('dp', 'fsdp'))
- cond_emb: bfloat16 [512, 1152], P(('dp', 'fsdp'))
- w_ada: bfloat16 [2, 1152, 6912], P(None, 'fsdp')
- b_ada: bfloat16 [2, 6912], replicated
- w_qkv: bfloat16 [2, 1152, 3456], P(None, 'fsdp')
- b_qkv: bfloat16 [2, 3456], replicated
- w_proj: bfloat16 [2, 1152, 1152], P(None, 'fsdp')
- b_proj: bfloat16 [2, 1152], replicated
- w_fc1: bfloat16 [2, 1152, 4608], P(None, 'fsdp')
- b_fc1: bfloat16 [2, 4608], replicated
- w_fc2: bfloat16 [2, 4608, 1152], P(None, 'fsdp')
- b_fc2: bfloat16 [2, 1152], replicated
Outputs:
- output: bfloat16 [512, 256, 1152], P(('dp', 'fsdp'))
All inputs are finite; a program needn't handle non-finite values.
Results may differ from a plain program's by a relative error of at most 0.0139485.
Values are sent between devices in bfloat16 or wider.
A program may use at most 1 GiB of HBM per device.

v0:
```python
import jax
import jax.numpy as jnp
from jax import lax
from jax.sharding import PartitionSpec as P

NUM_HEADS = 16
LN_EPS = 1e-6


def layer_norm(values_in):
    mean_val = jnp.mean(values_in, axis=-1, keepdims=True)
    centered = values_in - mean_val
    var_val = jnp.mean(centered * centered, axis=-1, keepdims=True)
    return centered * lax.rsqrt(var_val + LN_EPS)


def gather_rows(shard):
    return lax.all_gather(shard, 'fsdp', axis=0, tiled=True)


def value_a9(residual, modulation, w_qkv, b_qkv, w_proj, b_proj, w_fc1, b_fc1, w_fc2, b_fc2):
    samples, tokens, hidden = residual.shape
    head_dim = hidden // NUM_HEADS
    mod_parts = modulation.reshape(samples, 6, 1, hidden)
    shift_a = mod_parts[:, 0]
    scale_a = mod_parts[:, 1]
    gate_a = mod_parts[:, 2]
    shift_m = mod_parts[:, 3]
    scale_m = mod_parts[:, 4]
    gate_m = mod_parts[:, 5]
    resid_a = residual.astype(jnp.float32)
    normed = (layer_norm(resid_a) * (1.0 + scale_a) + shift_a).astype(jnp.bfloat16)
    full_qkv = gather_rows(w_qkv)
    qkv_rows = (jnp.einsum('toe,ef->tof', normed, full_qkv, preferred_element_type=jnp.float32) + b_qkv.astype(jnp.float32)).astype(jnp.bfloat16)
    qkv_rows = qkv_rows.reshape(samples, tokens, 3, NUM_HEADS, head_dim)
    scores = jnp.einsum('sqhd,skhd->shqk', qkv_rows[:, :, 0], qkv_rows[:, :, 1], preferred_element_type=jnp.float32) * (head_dim ** -0.5)
    attn_probs = jax.nn.softmax(scores, axis=-1).astype(jnp.bfloat16)
    attn_out = jnp.einsum('shqk,skhd->sqhd', attn_probs, qkv_rows[:, :, 2], preferred_element_type=jnp.float32).astype(jnp.bfloat16).reshape(samples, tokens, hidden)
    full_proj = gather_rows(w_proj)
    proj_out = jnp.einsum('toe,ef->tof', attn_out, full_proj, preferred_element_type=jnp.float32) + b_proj.astype(jnp.float32)
    resid_b = (resid_a + gate_a * proj_out).astype(jnp.bfloat16).astype(jnp.float32)
    normed_b = (layer_norm(resid_b) * (1.0 + scale_m) + shift_m).astype(jnp.bfloat16)
    full_fc1 = gather_rows(w_fc1)
    pre_act = jnp.einsum('toe,ef->tof', normed_b, full_fc1, preferred_element_type=jnp.float32) + b_fc1.astype(jnp.float32)
    hidden_act = jax.nn.gelu(pre_act, approximate=True).astype(jnp.bfloat16)
    full_fc2 = gather_rows(w_fc2)
    mlp_out = jnp.einsum('snf,fd->snd', hidden_act, full_fc2, preferred_element_type=jnp.float32) + b_fc2.astype(jnp.float32)
    return (resid_b + gate_m * mlp_out).astype(jnp.bfloat16)


def solution(mesh):
    batch_spec = P(('dp', 'fsdp'), None, None)
    cond_spec = P(('dp', 'fsdp'), None)
    shard_spec = P(None, 'fsdp', None)
    bias_spec = P(None, None)

    def local_run(latents, cond_emb, w_ada, b_ada, w_qkv, b_qkv, w_proj, b_proj, w_fc1, b_fc1, w_fc2, b_fc2):
        cond_act = jax.nn.silu(cond_emb.astype(jnp.float32)).astype(jnp.bfloat16)
        residual = latents
        for layer_idx in range(w_ada.shape[0]):
            full_ada = gather_rows(w_ada[layer_idx])
            modulation = jnp.dot(cond_act, full_ada, preferred_element_type=jnp.float32) + b_ada[layer_idx].astype(jnp.float32)
            modulation = modulation.astype(jnp.bfloat16).astype(jnp.float32)
            residual = value_a9(residual, modulation, w_qkv[layer_idx], b_qkv[layer_idx], w_proj[layer_idx], b_proj[layer_idx], w_fc1[layer_idx], b_fc1[layer_idx], w_fc2[layer_idx], b_fc2[layer_idx])
        return residual

    in_specs = (batch_spec, cond_spec, shard_spec, bias_spec, shard_spec, bias_spec, shard_spec, bias_spec, shard_spec, bias_spec, shard_spec, bias_spec)
    return jax.shard_map(local_run, mesh=mesh, in_specs=in_specs, out_specs=batch_spec, check_vma=False)
```

profile of v0, /device:TPU:1, one launch (start us, length us, event | category | flops | bytes accessed | tf_op | source)
XLA Modules:
  0.0 904.9 jit_solution(8061516387718670605)
XLA Ops:
  6.6 2.4 fusion.173
  9.1 1.9 fusion.178
  11.1 0.7 all-gather.31.cloned.1.call-update
  11.8 1.6 fusion.179
  13.4 2.0 fusion.174
  15.6 2.0 fusion.175
  17.6 0.7 all-gather.33.cloned.1.call-update
  18.4 0.7 all-gather.35.cloned.1.call-update
  19.1 0.7 all-gather.37.cloned.1.call-update
  20.4 1.0 convert_reduce_fusion.4
  21.4 0.9 convert_reduce_fusion.8
  22.7 0.8 fusion.104
  23.4 0.6 convert_reduce_fusion.11
  24.1 0.7 convert_reduce_fusion.6
  24.7 0.6 convert_reduce_fusion.10
  25.4 91.9 %all-gather.21.cloned.1.call-done = bf16[1,1152,6912]{2,0,1:T(2,128)(2,1)} async-done(((bf16[1,9,6912]{2,0,1:T(2,128)(2,1)}), bf16[1,1152,6912]{2,0,1:T(2,128)(2,1)}) %all-gather.21.cloned.1.call-update) | async-done | bytes 15925264 | tf_op jit(solution)/shard_map/all_gather | solution.py:18
  117.3 12.3 %fusion.69 = f32[4,6912]{1,0:T(4,128)S(1)} fusion(bf16[1,1152,6912]{2,0,1:T(2,128)(2,1)} %all-gather.21.cloned.1.call-done, f32[6912]{0:T(1024)S(1)} %get-tuple-element.6, bf16[4,1152]{1,0:T(4,128)(2,1)S(1)} %copy-done.5), kind=kOutput, calls=%fused_computation.61 | convolution fusion | flops 63811584 | bytes 16072704 | tf_op jit(solution)/shard_map/dot_general | solution.py:62
  129.7 68.4 %all-gather.23.cloned.1.call-done = bf16[1,1152,3456]{2,0,1:T(2,128)(2,1)} async-done(((bf16[1,9,3456]{2,0,1:T(2,128)(2,1)}), bf16[1,1152,3456]{2,0,1:T(2,128)(2,1)}) %all-gather.23.cloned.1.call-update) | async-done | bytes 7962640 | tf_op jit(solution)/shard_map/all_gather | solution.py:18
  198.2 17.8 %add_convert_fusion.1 = bf16[4,256,3456]{2,1,0:T(8,128)(2,1)} fusion(bf16[1,1152,3456]{2,0,1:T(2,128)(2,1)} %all-gather.23.cloned.1.call-done, f32[3456]{0:T(1024)S(1)} %get-tuple-element.10, bf16[4,256,1152]{2,1,0:T(8,128)(2,1)S(1)} %copy-done, f32[4,1152]{1,0:T(4,128)S(1)} %get-tuple-element.49, f32[4,1152]{1,0:T(4,128)S(1)} %get-tuple-element.50, ...), kind=kOutput, calls=%fused_computation.35 | convolution fusion | flops 8167882752 | bytes 17458688 | tf_op jit(solution)/shard_map/toe,ef->tof/dot_general | solution.py:34
  215.9 10.3 %copy.65 = bf16[4,256,3456]{1,2,0:T(8,128)(2,1)} copy(bf16[4,256,3456]{2,1,0:T(8,128)(2,1)} %add_convert_fusion.1) | data formatting | bytes 14155776 | tf_op jit(solution)/shard_map/convert_element_type | solution.py:34
  226.2 10.5 %fusion.131 = f32[4,16,256,256]{2,3,1,0:T(8,128)} fusion(bf16[4,256,3,16,72]{1,4,3,2,0:T(8,128)(2,1)} %bitcast.152), kind=kOutput, calls=%fused_computation.115 | convolution fusion | flops 603979776 | bytes 21495808 | tf_op jit(solution)/shard_map/sqhd,skhd->shqk/dot_general | solution.py:36
  236.7 19.4 %fusion.180 = (f32[4,16,256]{2,1,0:T(8,128)S(1)}, f32[4,16,256,256]{2,3,1,0:T(8,128)}) fusion(f32[4,16,256,256]{2,3,1,0:T(8,128)} %fusion.131), kind=kOutput, calls=%fused_computation.192 | output fusion | flops 16777472 | bytes 33619968 | tf_op jit(solution)/shard_map/sub | solution.py:37
  256.1 47.8 %all-gather.31.cloned.1.call-done = bf16[1,1152,6912]{2,0,1:T(2,128)(2,1)} async-done(((bf16[1,9,6912]{2,0,1:T(2,128)(2,1)}), bf16[1,1152,6912]{2,0,1:T(2,128)(2,1)}) %all-gather.31.cloned.1.call-update) | async-done | bytes 15925264 | tf_op jit(solution)/shard_map/all_gather | solution.py:18
  303.9 12.3 %fusion.63 = f32[4,6912]{1,0:T(4,128)S(1)} fusion(bf16[1,1152,6912]{2,0,1:T(2,128)(2,1)} %all-gather.31.cloned.1.call-done, f32[6912]{0:T(1024)S(1)} %get-tuple-element.5, bf16[4,1152]{1,0:T(4,128)(2,1)S(1)} %copy-done.5), kind=kOutput, calls=%fused_computation.59 | convolution fusion | flops 63811584 | bytes 16072704 | tf_op jit(solution)/shard_map/dot_general | solution.py:62
  316.3 9.5 %fusion.157 = bf16[4,16,72,256]{3,2,1,0:T(8,128)(2,1)} fusion(f32[4,16,256,256]{2,3,1,0:T(8,128)} %get-tuple-element.38, f32[4,16,256]{2,1,0:T(8,128)S(1)} %get-tuple-element.37, bf16[4,256,3,16,72]{1,4,3,2,0:T(8,128)(2,1)} %bitcast.153), kind=kOutput, calls=%fused_computation.135 | convolution fusion | flops 613548032 | bytes 21561344 | tf_op jit(solution)/shard_map/shqk,skhd->sqhd/dot_general | solution.py:38
  325.8 48.0 %all-gather.25.cloned.1.call-done = bf16[1,1152,1152]{2,0,1:T(2,128)(2,1)} async-done(((bf16[1,9,1152]{2,0,1:T(2,128)(2,1)}), bf16[1,1152,1152]{2,0,1:T(2,128)(2,1)}) %all-gather.25.cloned.1.call-update) | async-done | bytes 2654224 | tf_op jit(solution)/shard_map/all_gather | solution.py:18
  373.8 7.4 convert_reduce_fusion.2
  381.3 1.4 copy-done.3
  382.6 0.8 fusion.100
  383.4 77.4 %all-gather.27.cloned.1.call-done = bf16[1,1152,4608]{2,0,1:T(2,128)(2,1)} async-done(((bf16[1,9,4608]{2,0,1:T(2,128)(2,1)}), bf16[1,1152,4608]{2,0,1:T(2,128)(2,1)}) %all-gather.27.cloned.1.call-update) | async-done | bytes 10616848 | tf_op jit(solution)/shard_map/all_gather | solution.py:18
  460.8 24.5 %fusion.9.clone.1.clone.4 = bf16[4,256,4608]{2,1,0:T(8,128)(2,1)} fusion(bf16[1,1152,4608]{2,0,1:T(2,128)(2,1)} %all-gather.27.cloned.1.call-done, f32[4608]{0:T(1024)S(1)} %get-tuple-element.8, bf16[4,256,1152]{2,1,0:T(8,128)(2,1)} %copy-done.3, f32[4,1152]{1,0:T(4,128)S(1)} %get-tuple-element.47, ...), kind=kOutput, calls=%fused_computation.11.clone.clone.clone.clone.clone.1 | convolution fusion | flops 10925899776 | bytes 22476800 | tf_op jit(solution)/shard_map/toe,ef->tof/dot_general | solution.py:44
  485.3 64.4 %all-gather.29.cloned.1.call-done = bf16[1,4608,1152]{2,0,1:T(2,128)(2,1)} async-done(((bf16[1,36,1152]{2,0,1:T(2,128)(2,1)}), bf16[1,4608,1152]{2,0,1:T(2,128)(2,1)}) %all-gather.29.cloned.1.call-update) | async-done | bytes 10616848 | tf_op jit(solution)/shard_map/all_gather | solution.py:18
  549.7 21.5 %convert_reduce_fusion.1 = (f32[4,256]{1,0:T(4,128)S(1)}, bf16[4,256,1152]{2,1,0:T(8,128)(2,1)S(1)}) fusion(f32[1152]{0:T(1024)S(1)} %get-tuple-element.12, bf16[1,4608,1152]{2,0,1:T(2,128)(2,1)} %all-gather.29.cloned.1.call-done, bf16[4,256,1152]{2,1,0:T(8,128)(2,1)} %copy-done.3, f32[4,1152]{1,0:T(4,128)S(1)} %bitcast.156, ...), kind=kOutput, calls=%fused_computation.67 | convolution fusion | flops 10879892480 | bytes 24799744 | tf_op jit(solution)/shard_map/snf,fd->snd/dot_general | solution.py:47
  571.2 0.8 fusion.96
  572.1 58.6 %all-gather.33.cloned.1.call-done = bf16[1,1152,3456]{2,0,1:T(2,128)(2,1)} async-done(((bf16[1,9,3456]{2,0,1:T(2,128)(2,1)}), bf16[1,1152,3456]{2,0,1:T(2,128)(2,1)}) %all-gather.33.cloned.1.call-update) | async-done | bytes 7962640 | tf_op jit(solution)/shard_map/all_gather | solution.py:18
  630.7 17.9 %add_convert_fusion = bf16[4,256,3456]{2,1,0:T(8,128)(2,1)} fusion(bf16[1,1152,3456]{2,0,1:T(2,128)(2,1)} %all-gather.33.cloned.1.call-done, f32[3456]{0:T(1024)S(1)} %get-tuple-element.9, bf16[4,256,1152]{2,1,0:T(8,128)(2,1)S(1)} %get-tuple-element.42, f32[4,1152]{1,0:T(4,128)S(1)} %get-tuple-element.53, f32[4,1152]{1,0:T(4,128)S(1)} %get-tuple-element.54, ...), kind=kOutput, calls=%fused_computation.34 | convolution fusion | flops 8167882752 | bytes 17458688 | tf_op jit(solution)/shard_map/toe,ef->tof/dot_general | solution.py:34
  648.6 10.2 %copy.71 = bf16[4,256,3456]{1,2,0:T(8,128)(2,1)} copy(bf16[4,256,3456]{2,1,0:T(8,128)(2,1)} %add_convert_fusion) | data formatting | bytes 14155776 | tf_op jit(solution)/shard_map/convert_element_type | solution.py:34
  658.9 10.5 %fusion.130 = f32[4,16,256,256]{2,3,1,0:T(8,128)} fusion(bf16[4,256,3,16,72]{1,4,3,2,0:T(8,128)(2,1)} %bitcast.154), kind=kOutput, calls=%fused_computation.111 | convolution fusion | flops 603979776 | bytes 21495808 | tf_op jit(solution)/shard_map/sqhd,skhd->shqk/dot_general | solution.py:36
  669.4 19.3 %fusion.185 = (f32[4,16,256]{2,1,0:T(8,128)S(1)}, f32[4,16,256,256]{2,3,1,0:T(8,128)}) fusion(f32[4,16,256,256]{2,3,1,0:T(8,128)} %fusion.130), kind=kOutput, calls=%fused_computation.193 | output fusion | flops 16777472 | bytes 33619968 | tf_op jit(solution)/shard_map/sub | solution.py:37
  688.7 9.5 %fusion.156 = bf16[4,16,72,256]{3,2,1,0:T(8,128)(2,1)} fusion(f32[4,16,256,256]{2,3,1,0:T(8,128)} %get-tuple-element.44, f32[4,16,256]{2,1,0:T(8,128)S(1)} %get-tuple-element.43, bf16[4,256,3,16,72]{1,4,3,2,0:T(8,128)(2,1)} %bitcast.155), kind=kOutput, calls=%fused_computation.134 | convolution fusion | flops 613548032 | bytes 21561344 | tf_op jit(solution)/shard_map/shqk,skhd->sqhd/dot_general | solution.py:38
  698.2 2.6 all-gather.35.cloned.1.call-done
  700.9 7.4 convert_reduce_fusion
  708.3 1.4 copy-done.1
  709.7 0.8 fusion.92
  710.5 77.5 %all-gather.37.cloned.1.call-done = bf16[1,1152,4608]{2,0,1:T(2,128)(2,1)} async-done(((bf16[1,9,4608]{2,0,1:T(2,128)(2,1)}), bf16[1,1152,4608]{2,0,1:T(2,128)(2,1)}) %all-gather.37.cloned.1.call-update) | async-done | bytes 10616848 | tf_op jit(solution)/shard_map/all_gather | solution.py:18
  788.0 27.3 %fusion.17.clone.4 = bf16[4,256,4608]{2,1,0:T(8,128)(2,1)} fusion(bf16[1,1152,4608]{2,0,1:T(2,128)(2,1)} %all-gather.37.cloned.1.call-done, f32[4608]{0:T(1024)S(1)} %copy-done.6, bf16[4,256,1152]{2,1,0:T(8,128)(2,1)} %copy-done.1, f32[4,1152]{1,0:T(4,128)S(1)} %get-tuple-element.51, f32[4,1152]{1,0:T(4,128)S(1)} %get-tuple-element.52, ...), kind=kOutput, calls=%fused_computation.19.clone.clone.clone.1 | convolution fusion | flops 10925899776 | bytes 22476800 | tf_op jit(solution)/shard_map/toe,ef->tof/dot_general | solution.py:44
  815.3 61.6 %all-gather.39.cloned.1.call-done = bf16[1,4608,1152]{2,0,1:T(2,128)(2,1)} async-done(((bf16[1,36,1152]{2,0,1:T(2,128)(2,1)}), bf16[1,4608,1152]{2,0,1:T(2,128)(2,1)}) %all-gather.39.cloned.1.call-update) | async-done | bytes 10616848 | tf_op jit(solution)/shard_map/all_gather | solution.py:18
  876.9 20.7 %fusion.111 = bf16[4,256,1152]{2,1,0:T(8,128)(2,1)} fusion(bf16[4,256,1152]{2,1,0:T(8,128)(2,1)S(1)} %copy-done.2, bf16[1,4608,1152]{2,0,1:T(2,128)(2,1)} %all-gather.39.cloned.1.call-done, f32[1152]{0:T(1024)S(1)} %copy-done.9, f32[4,1152]{1,0:T(4,128)S(1)} %bitcast.157, bf16[4,256,4608]{2,1,0:T(8,128)(2,1)} %fusion.17.clone.4), kind=kOutput, calls=%fused_computation.105 | convolution fusion | flops 10877534208 | bytes 24795648 | tf_op jit(solution)/shard_map/snf,fd->snd/dot_general | solution.py:47
  (57 shorter events, 1.8 us)
Async XLA Ops:
  6.5 15.7 %copy-start = (bf16[4,256,1152]{2,1,0:T(8,128)(2,1)S(1)}, bf16[4,256,1152]{2,1,0:T(8,128)(2,1)}, u32[]{:S(2)}) copy-start(bf16[4,256,1152]{2,1,0:T(8,128)(2,1)} %param.12) | copy-start | bytes 7077892
  6.5 16.9 %copy-start.7 = (bf16[2,1152]{1,0:T(2,128)(2,1)S(1)}, bf16[2,1152]{1,0:T(2,128)(2,1)}, u32[]{:S(2)}) copy-start(bf16[2,1152]{1,0:T(2,128)(2,1)} %param.19) | copy-start | bytes 13828
  6.5 17.5 %copy-start.4 = (bf16[2,4608]{1,0:T(2,128)(2,1)S(1)}, bf16[2,4608]{1,0:T(2,128)(2,1)}, u32[]{:S(2)}) copy-start(bf16[2,4608]{1,0:T(2,128)(2,1)} %param.21) | copy-start | bytes 55300
  6.5 18.2 %copy-start.8 = (bf16[2,1152]{1,0:T(2,128)(2,1)S(1)}, bf16[2,1152]{1,0:T(2,128)(2,1)}, u32[]{:S(2)}) copy-start(bf16[2,1152]{1,0:T(2,128)(2,1)} %param.23) | copy-start | bytes 13828
  6.5 110.7 %copy-start.5 = (bf16[4,1152]{1,0:T(4,128)(2,1)S(1)}, bf16[4,1152]{1,0:T(4,128)(2,1)}, u32[]{:S(2)}) copy-start(bf16[4,1152]{1,0:T(4,128)(2,1)} %param.13) | copy-start | bytes 27652
  6.5 110.7 %all-gather.21.cloned.1.call-start = ((), (), s32[]{:S(2)}) async-start(), calls=%async_computation | async-start | bytes 32099328 | tf_op jit(solution)/shard_map/all_gather | solution.py:18
  9.0 189.1 %all-gather.23.cloned.1.call-start = ((), (), s32[]{:S(2)}) async-start(), calls=%async_computation.1 | async-start | bytes 16049664 | tf_op jit(solution)/shard_map/all_gather | solution.py:18
  11.0 292.9 %all-gather.31.cloned.1.call-start = ((), (), s32[]{:S(2)}) async-start(), calls=%async_computation.5 | async-start | bytes 32099328 | tf_op jit(solution)/shard_map/all_gather | solution.py:18
  11.8 362.1 %all-gather.25.cloned.1.call-start = ((), (), s32[]{:S(2)}) async-start(), calls=%async_computation.2 | async-start | bytes 5349888 | tf_op jit(solution)/shard_map/all_gather | solution.py:18
  13.4 447.4 %all-gather.27.cloned.1.call-start = ((), (), s32[]{:S(2)}) async-start(), calls=%async_computation.3 | async-start | bytes 21399552 | tf_op jit(solution)/shard_map/all_gather | solution.py:18
  15.5 534.2 %all-gather.29.cloned.1.call-start = ((), (), s32[]{:S(2)}) async-start(), calls=%async_computation.4 | async-start | bytes 21399552 | tf_op jit(solution)/shard_map/all_gather | solution.py:18
  17.6 613.1 %all-gather.33.cloned.1.call-start = ((), (), s32[]{:S(2)}) async-start(), calls=%async_computation.6 | async-start | bytes 16049664 | tf_op jit(solution)/shard_map/all_gather | solution.py:18
  18.3 682.5 %all-gather.35.cloned.1.call-start = ((), (), s32[]{:S(2)}) async-start(), calls=%async_computation.7 | async-start | bytes 5349888 | tf_op jit(solution)/shard_map/all_gather | solution.py:18
  19.1 768.9 %all-gather.37.cloned.1.call-start = ((), (), s32[]{:S(2)}) async-start(), calls=%async_computation.8 | async-start | bytes 21399552 | tf_op jit(solution)/shard_map/all_gather | solution.py:18
  19.8 857.1 %all-gather.39.cloned.1.call-start = ((), (), s32[]{:S(2)}) async-start(), calls=%async_computation.9 | async-start | bytes 21399552 | tf_op jit(solution)/shard_map/all_gather | solution.py:18
  381.2 1.4 copy-start.3
  688.7 12.1 %copy-start.10 = (f32[1152]{0:T(1024)S(1)}, f32[1152]{0:T(1024)}, u32[]{:S(2)}) copy-start(f32[1152]{0:T(1024)} %get-tuple-element.13) | copy-start | bytes 13828
  700.9 87.1 %copy-start.6 = (f32[4608]{0:T(1024)S(1)}, f32[4608]{0:T(1024)}, u32[]{:S(2)}) copy-start(f32[4608]{0:T(1024)} %get-tuple-element.7) | copy-start | bytes 55300
  708.3 1.4 copy-start.1
  788.0 88.9 %copy-start.2 = (bf16[4,256,1152]{2,1,0:T(8,128)(2,1)S(1)}, bf16[4,256,1152]{2,1,0:T(8,128)(2,1)}, u32[]{:S(2)}) copy-start(bf16[4,256,1152]{2,1,0:T(8,128)(2,1)} %copy-done.1) | copy-start | bytes 7077892
  788.0 88.9 %copy-start.9 = (f32[1152]{0:T(1024)S(1)}, f32[1152]{0:T(1024)}, u32[]{:S(2)}) copy-start(f32[1152]{0:T(1024)} %get-tuple-element.11) | copy-start | bytes 13828
Sparse Core Ops, SparseCore 0:
  10.3 106.8 all-gather.20
  120.4 77.7 all-gather.22
  201.1 102.7 all-gather.30
  306.8 67.0 all-gather.24
  376.6 84.1 all-gather.26
  463.6 86.0 all-gather.28
  552.9 77.8 all-gather.32
  633.7 67.1 all-gather.34
  703.8 84.1 all-gather.36
  790.8 86.0 all-gather.38
where the time goes:
time: 915 us; the launch traced here: 905 us
  waiting for transfers between devices  602 us (66%)
  matrix products  209 us (23%)
  other arithmetic  46.2 us (5%)
  local copies, waits for them, and re-layouts  33.4 us (4%)
  between operations  14.2 us (2%)
    all_gather x10, waiting for transfers between devices, gather_rows(): return lax.all_gather(shard, 'fsdp', axis=0, tiled=True)  598 us
    dot_general x2, matrix products, value_a9(): jnp.einsum('toe,ef->tof', normed_b, full_fc1, preferred_element_type=jnp....  51.9 us
    dot_general x2, matrix products, value_a9(): jnp.einsum('snf,fd->snd', hidden_act, full_fc2, preferred_element_type=jn...  42.1 us
    sub x2, other arithmetic, value_a9(): attn_probs = jax.nn.softmax(scores, axis=-1).astype(jnp.bfloat16)  38.7 us
    dot_general x2, matrix products, value_a9(): jnp.einsum('toe,ef->tof', normed, full_qkv, preferred_element_type=jnp.fl...  35.7 us
    dot_general x2, matrix products, local_run(): jnp.dot(cond_act, full_ada, preferred_element_type=jnp.float32)  24.6 us
    dot_general x2, matrix products, value_a9(): jnp.einsum('sqhd,skhd->shqk', qkv_rows[:, :, 0], qkv_rows[:, :, 1], prefe...  21 us
    convert_element_type x2, local copies, waits for them, and re-layouts, value_a9(): (jnp.einsum('toe,ef->tof', normed, full_qkv, preferred_element_type=jnp.f...  20.5 us
  transfers between devices with their start and end apart: 10, of which 10 were waited for; matrix products, arithmetic and copies ran while one was open for 29% of the time, Pallas kernels for 0%

commit v1 on v0

v1 whole, which is shorter than its diff:
```python
import functools
import jax
import jax.numpy as jnp
from jax import lax
from jax.experimental import pallas as pl
from jax.experimental.pallas import tpu as pltpu
from jax.sharding import PartitionSpec

MESH = pl.DeviceIdType.MESH
NL = 2
LANE = 128
RING, GROUP = 4, 8
RUN, PLANE, HALF = 72, 288, 144
TILE, QT = 256, 512
F2_COLS = 5 * LANE
N_A = 4608
CUT_A = ((3, 2, 1), (2, 3, 1))
CUT_B = ((2, 3, 1),)
CUT_C = ((7, 7, 1),)
CUT_D = ((3, 2, 1),)
SUBS = {(l, k): cut for l, row in enumerate(((CUT_A, CUT_A, CUT_B), (CUT_A, CUT_C, CUT_D))) for k, cut in enumerate(row)}
STARTS = (3, 17, 31, 47, 71, 99, 3, 58)
COLOURS = (1, 2, 0)


def width(l, k):
    return LANE * sum(a + b + c for a, b, c in SUBS[l, k])


W_MOD = 7 * LANE
W_F2 = F2_COLS + LANE


class Pos:
    def __init__(self):
        me = lax.axis_index('fsdp')
        self.c = lax.rem(me, 2)
        self.x = lax.rem(me // 2, RING)
        self.y = lax.rem(me // GROUP, RING)
        self.z = me // 32

    def dev(self, z=None, y=None, x=None, c=None):
        z = self.z if z is None else z
        y = self.y if y is None else y
        x = self.x if x is None else x
        c = self.c if c is None else c
        return {'fsdp': ((z * RING + y) * RING + x) * 2 + c}


def step4(v, k):
    return lax.rem(v + (k + RING), RING)


class Comm:
    def __init__(self, ssem, rsem):
        self.ssem, self.rsem, self.n = ssem, rsem, 0

    def take(self, k):
        b = self.n
        self.n += k
        return b

    def copy(self, src, dst, i, dev):
        return pltpu.make_async_remote_copy(src_ref=src, dst_ref=dst, send_sem=self.ssem.at[i], recv_sem=self.rsem.at[i], device_id=dev, device_id_type=MESH)


class Ring:
    def __init__(self, comm, pos, axis, sel, half):
        self.comm, self.sel, self.half = comm, sel, half
        self.b = comm.take(RING)
        me = getattr(pos, axis)
        self.me, self.r, self.l, self.o = me, step4(me, 1), step4(me, -1), step4(me, 2)
        self.right, self.left = pos.dev(**{axis: self.r}), pos.dev(**{axis: self.l})

    def start(self):
        own = self.sel(self.me)
        self.comm.copy(own, own, self.b, self.right).start()
        self.comm.copy(own, own, self.b + 1, self.left).start()

    def mid(self):
        a = self.sel(self.l)
        self.comm.copy(a, a, self.b, self.right).wait_recv()
        h = self.half(self.l, 0)
        self.comm.copy(h, h, self.b + 2, self.right).start()
        a = self.sel(self.r)
        self.comm.copy(a, a, self.b + 1, self.left).wait_recv()
        h = self.half(self.r, 1)
        self.comm.copy(h, h, self.b + 3, self.left).start()

    def end(self):
        h = self.half(self.o, 0)
        self.comm.copy(h, h, self.b + 2, self.right).wait_recv()
        h = self.half(self.o, 1)
        self.comm.copy(h, h, self.b + 3, self.left).wait_recv()

    def drain(self):
        own = self.sel(self.me)
        self.comm.copy(own, own, self.b, self.right).wait_send()
        self.comm.copy(own, own, self.b + 1, self.left).wait_send()
        h = self.half(self.l, 0)
        self.comm.copy(h, h, self.b + 2, self.right).wait_send()
        h = self.half(self.r, 1)
        self.comm.copy(h, h, self.b + 3, self.left).wait_send()


def pack_unit(comm, pos, g, off, wa, wb, wc):
    base = pos.c * (N_A // 2) + off
    ca = pl.ds(pl.multiple_of(base, LANE), wa)
    cb = pl.ds(pl.multiple_of(base + wa, LANE), wb)

    def cc(i):
        return pl.ds(pl.multiple_of(base + wa + wb + i * wc, LANE), wc)

    x, y, z = pos.x, pos.y, pos.z
    two = (pl.ds(0, 2), pl.ds(2, 2))
    big = (pl.ds(0, HALF), pl.ds(HALF, HALF))
    rings_a = [Ring(comm, pos, 'y', lambda i: g.at[z, rows_of(i), ca], lambda i, h: g.at[z, rows_of(i, h), ca]),
               Ring(comm, pos, 'z', lambda i: g.at[i, :, ca], lambda i, h: g.at[i, big[h], ca])]
    rings_b = [Ring(comm, pos, 'z', lambda i: g.at[i, rows_of(y), cb], lambda i, h: g.at[i, rows_of(y, h), cb]),
               Ring(comm, pos, 'y', lambda i: g.at[:, rows_of(i), cb], lambda i, h: g.at[two[h], rows_of(i), cb])]
    rings_c = [Ring(comm, pos, 'y', lambda i: g.at[z, rows_of(i), cc(x)], lambda i, h: g.at[z, rows_of(i, h), cc(x)]),
               Ring(comm, pos, 'z', lambda i: g.at[i, :, cc(x)], lambda i, h: g.at[i, big[h], cc(x)]),
               Ring(comm, pos, 'x', lambda i: g.at[:, :, cc(i)], lambda i, h: g.at[two[h], :, cc(i)])]
    def across(c):
        b = c * (N_A // 2) + off
        return [g.at[:, :, pl.ds(pl.multiple_of(b + o, LANE), n)] for o, n in ((0, wa), (wa, wb), (wa + wb, RING * wc))]

    return (rings_a, rings_b, rings_c), across(pos.c), across(1 - pos.c)


def rows_of(y, h=None):
    o, n = {None: (0, RUN), 0: (0, 40), 1: (40, 32)}[h]
    return pl.ds(pl.multiple_of(y * RUN + o, GROUP), n)


def fc2_unit(comm, pos, g, wa):
    r0 = pos.c * HALF
    x, y, z = pos.x, pos.y, pos.z
    full = pl.ds(pl.multiple_of(r0, GROUP), HALF)
    rows = (pl.ds(pl.multiple_of(r0, GROUP), RUN), pl.ds(pl.multiple_of(r0 + RUN, GROUP), RUN))
    two = (pl.ds(0, 2), pl.ds(2, 2))
    ca, cb = pl.ds(0, wa), pl.ds(wa, F2_COLS - wa)

    def cc(i):
        return pl.ds(pl.multiple_of(F2_COLS + i * LANE, LANE), LANE)

    rings_a = [Ring(comm, pos, 'y', lambda i: g.at[z, i, full, ca], lambda i, h: g.at[z, i, rows[h], ca]),
               Ring(comm, pos, 'z', lambda i: g.at[i, :, full, ca], lambda i, h: g.at[i, two[h], full, ca])]
    rings_b = [Ring(comm, pos, 'z', lambda i: g.at[i, y, full, cb], lambda i, h: g.at[i, y, rows[h], cb]),
               Ring(comm, pos, 'y', lambda i: g.at[:, i, full, cb], lambda i, h: g.at[two[h], i, full, cb])]
    rings_c = [Ring(comm, pos, 'y', lambda i: g.at[z, i, full, cc(x)], lambda i, h: g.at[z, i, rows[h], cc(x)]),
               Ring(comm, pos, 'z', lambda i: g.at[i, :, full, cc(x)], lambda i, h: g.at[i, two[h], full, cc(x)]),
               Ring(comm, pos, 'x', lambda i: g.at[:, :, full, cc(i)], lambda i, h: g.at[two[h], :, full, cc(i)])]
    def across(c):
        r = pl.ds(pl.multiple_of(c * HALF, GROUP), HALF)
        return [g.at[:, :, r, k] for k in (ca, cb, pl.ds(F2_COLS, RING * LANE))]

    return (rings_a, rings_b, rings_c), across(pos.c), across(1 - pos.c)


class Unit:
    def __init__(self, comm, pos, parts):
        self.rings, self.mine, self.other = parts
        self.comm = comm
        self.k = comm.take(3)
        self.sib = pos.dev(c=1 - pos.c)

    def across(self, i, refs):
        return self.comm.copy(refs[i], refs[i], self.k + i, self.sib)

    def stage(self, i, n):
        r = self.rings[i]
        if n == 2 * len(r):
            r[-1].end()
            self.across(i, self.mine).start()
        elif n == 2 * len(r) + 1:
            self.across(i, self.other).wait_recv()
        elif n % 2:
            r[n // 2].mid()
        else:
            if n:
                r[n // 2 - 1].end()
            r[n // 2].start()

    def drain(self):
        for i in range(3):
            for r in self.rings[i]:
                r.drain()
            self.across(i, self.mine).wait_send()


def mod_rings(comm, pos, h):
    y, z = pos.y, pos.z
    two, big = (pl.ds(0, 2), pl.ds(2, 2)), (pl.ds(0, HALF), pl.ds(HALF, HALF))
    ca, cb = pl.ds(0, RING * LANE), pl.ds(RING * LANE, 3 * LANE)
    return ([Ring(comm, pos, 'z', lambda i: h.at[i, rows_of(y), ca], lambda i, k: h.at[i, rows_of(y, k), ca]),
             Ring(comm, pos, 'y', lambda i: h.at[:, rows_of(i), ca], lambda i, k: h.at[two[k], rows_of(i), ca])],
            [Ring(comm, pos, 'y', lambda i: h.at[z, rows_of(i), cb], lambda i, k: h.at[z, rows_of(i, k), cb]),
             Ring(comm, pos, 'z', lambda i: h.at[i, :, cb], lambda i, k: h.at[i, big[k], cb])])


def entry_barrier(pos):
    bar = pltpu.get_barrier_semaphore()
    peers = [pos.dev(x=step4(pos.x, k)) for k in (1, 2, 3)]
    peers += [pos.dev(x=step4(pos.x, k), c=1 - pos.c) for k in (0, 1, 2, 3)]
    peers += [pos.dev(y=step4(pos.y, k)) for k in (1, -1)]
    peers += [pos.dev(z=step4(pos.z, k)) for k in (1, -1)]
    for p in peers:
        pl.semaphore_signal(bar, inc=1, device_id=p, device_id_type=MESH)
    pl.semaphore_wait(bar, len(peers))


HIDDEN = 1152
ROWS = 1024
HEAD = 72
HEADS = 16
LN_EPS = 1e-6
LOG2E = 1.4426950408889634


def ln_mod(v, shift, scale):
    mean = jnp.mean(v, axis=-1, keepdims=True)
    cen = v - mean
    var = jnp.mean(cen * cen, axis=-1, keepdims=True)
    return ((cen * lax.rsqrt(var + LN_EPS)) * (1.0 + scale) + shift).astype(jnp.bfloat16)


def piece(m_ref, l, s, j):
    return m_ref[l, pl.ds(s, 1), j * HIDDEN:(j + 1) * HIDDEN]


LT = 128


def norm1(src, m_ref, l, u):
    def body(i, _):
        rows = pl.ds(pl.multiple_of(i * LT, LT), LT)
        s = i // (TILE // LT)
        u[rows, :] = ln_mod(src[rows, :].astype(jnp.float32), piece(m_ref, l, s, 0), piece(m_ref, l, s, 1))
        return 0
    lax.fori_loop(0, ROWS // LT, body, 0)


def qkv_tiles(u, w, b, l, big, tick):
    def tile(cols, width):
        wt = w[:, :, cols].reshape(HIDDEN, width)
        for r in range(0, ROWS, QT):
            acc = jnp.dot(u[r:r + QT, :], wt, preferred_element_type=jnp.float32)
            big[r:r + QT, cols] = (acc + b[l:l + 1, cols].astype(jnp.float32)).astype(jnp.bfloat16)

    def body(n, _):
        tile(pl.ds(pl.multiple_of(n * QT, QT), QT), QT)
        tick(n)
        return 0
    lax.fori_loop(0, 6, body, 0)
    tile(slice(6 * QT, 6 * QT + 384), 384)


def attend(big, o, tick, n=RING):
    lane = lax.broadcasted_iota(jnp.int32, (1, TILE), 1)
    cst = (HEAD ** -0.5) * LOG2E

    def body(s, _):
        rows = pl.ds(pl.multiple_of(s * TILE, TILE), TILE)
        cur, cur_t = None, -1
        for h in range(HEADS):
            st = HEAD * h
            t0 = st // LANE
            off = st - t0 * LANE
            wd = LANE if off + HEAD <= LANE else 2 * LANE
            lo = t0 * LANE
            keep = jnp.logical_and(lane[:, :wd] >= off, lane[:, :wd] < off + HEAD)
            msk = jnp.where(keep, 1.0, 0.0).astype(jnp.bfloat16)
            q = big[rows, lo:lo + wd] * msk
            k = big[rows, HIDDEN + lo:HIDDEN + lo + wd]
            v = big[rows, 2 * HIDDEN + lo:2 * HIDDEN + lo + wd]
            sc = lax.dot_general(q, k, (((1,), (1,)), ((), ())), preferred_element_type=jnp.float32)
            mx = jnp.max(sc, axis=-1, keepdims=True)
            e = jnp.exp2((sc - mx) * cst)
            inv = 1.0 / jnp.sum(e, axis=-1, keepdims=True)
            p = (e * inv).astype(jnp.bfloat16)
            r = jnp.dot(p, v, preferred_element_type=jnp.float32)
            first = r[:, :LANE]
            if cur_t == t0 and off > 0:
                first = jnp.where(lane[:, :LANE] >= off, first, cur)
            if wd == LANE:
                cur, cur_t = first, t0
                if off + HEAD == LANE:
                    o[rows, lo:lo + LANE] = cur.astype(jnp.bfloat16)
                    cur, cur_t = None, -1
            else:
                o[rows, lo:lo + LANE] = first.astype(jnp.bfloat16)
                cur, cur_t = r[:, LANE:], t0 + 1
        tick(s)
        return 0
    lax.fori_loop(0, n, body, 0)


def proj_tiles(o, w, b, m_ref, l, src, x1, u, tick):
    def body(s, _):
        rows = pl.ds(pl.multiple_of(s * TILE, TILE), TILE)
        y = jnp.dot(o[rows, :], w[:, :, 3 * HIDDEN:].reshape(HIDDEN, HIDDEN), preferred_element_type=jnp.float32) + b[l:l + 1, :].astype(jnp.float32)
        v = (src[rows, :].astype(jnp.float32) + piece(m_ref, l, s, 2) * y).astype(jnp.bfloat16)
        x1[rows, :] = v
        u[rows, :] = ln_mod(v.astype(jnp.float32), piece(m_ref, l, s, 3), piece(m_ref, l, s, RING))
        tick(s)
        return 0
    lax.fori_loop(0, RING, body, 0)


def gelu(v):
    return 0.5 * v * (1.0 + jnp.tanh(0.7978845608028654 * (v + 0.044715 * (v * v * v))))


def fc1_tiles(u, w, b, l, big, tick):
    def body(n, _):
        cols = pl.ds(pl.multiple_of(n * QT, QT), QT)
        wt = w[:, :, cols].reshape(HIDDEN, QT)
        for r in range(0, ROWS, QT):
            acc = jnp.dot(u[r:r + QT, :], wt, preferred_element_type=jnp.float32)
            big[r:r + QT, cols] = gelu(acc + b[l:l + 1, cols].astype(jnp.float32)).astype(jnp.bfloat16)
        tick(n)
        return 0
    lax.fori_loop(0, 9, body, 0)


def fc2_tiles(big, w, b, m_ref, l, x1, dst, tick):
    def body(s, _):
        rows = pl.ds(pl.multiple_of(s * TILE, TILE), TILE)
        y = jnp.dot(big[rows, :], w[...].reshape(RING * HIDDEN, HIDDEN), preferred_element_type=jnp.float32) + b[l:l + 1, :].astype(jnp.float32)
        dst[rows, :] = (x1[rows, :].astype(jnp.float32) + piece(m_ref, l, s, 5) * y).astype(jnp.bfloat16)
        tick(s)
        return 0
    lax.fori_loop(0, RING, body, 0)


class Fan:
    def __init__(self, comm, pos, src, dst):
        self.comm, self.pos, self.src, self.dst = comm, pos, src, dst
        self.b = comm.take(GROUP)
        self.p = pos.x * 2 + pos.c

    def peer(self, k):
        q = lax.rem(self.p + k + GROUP, GROUP)
        return q, self.pos.dev(x=q // 2, c=lax.rem(q, 2))

    def put(self, k):
        q, dev = self.peer(k)
        return self.comm.copy(self.src(q), self.dst.at[self.p], self.b + k, dev)

    def start(self):
        for k in ORDER:
            self.put(k).start()

    def wait(self):
        for k in ORDER:
            q, dev = self.peer(-k)
            self.comm.copy(self.src(q), self.dst.at[q], self.b + k, dev).wait_recv()

    def drain(self):
        for k in ORDER:
            self.put(k).wait_send()


ORDER = range(1, GROUP)


class Scatter:
    def __init__(self, comm, pos, pieces, dst):
        self.comm, self.pos, self.pieces, self.dst = comm, pos, pieces, dst
        self.n = len(pieces(0, 0, 0))
        self.b = comm.take(GROUP * self.n)

    def each(self):
        for c in range(2):
            for d in (1, 3, 2, 0):
                x = step4(self.pos.x, d)
                for i, (src, at) in enumerate(self.pieces(x, c, self.pos.c)):
                    yield c, d, i, x, src, at

    def ends(self, d, i, at):
        return self.dst.at[2 * self.pos.x + self.pos.c, :, at], self.comm.rsem.at[self.b + (self.pos.c * RING + d) * self.n + i]

    def far(self, c, d, i, x, src, at):
        dst, r = self.ends(d, i, at)
        return pltpu.make_async_remote_copy(src_ref=src, dst_ref=dst, send_sem=self.comm.ssem.at[self.b + (c * RING + d) * self.n + i], recv_sem=r,
                                            device_id=self.pos.dev(x=x, c=c), device_id_type=MESH)

    def near(self, c, d, i, x, src, at):
        return pltpu.make_async_copy(src, *self.ends(d, i, at))

    def start(self):
        for v in self.each():
            if v[1]:
                self.far(*v).start()
            else:
                pl.when(self.pos.c != v[0])(lambda v=v: self.far(*v).start())
                pl.when(self.pos.c == v[0])(lambda v=v: self.near(*v).start())

    def wait(self):
        for c, d, i, x, src, at in self.each():
            dst = self.dst.at[2 * step4(self.pos.x, -d) + c, :, at]
            pltpu.make_async_copy(src, dst, self.comm.rsem.at[self.b + (c * RING + d) * self.n + i]).wait()

    def drain(self):
        for v in self.each():
            if v[1]:
                self.far(*v).wait_send()
            else:
                pl.when(self.pos.c != v[0])(lambda v=v: self.far(*v).wait_send())


class Scatter2:
    def __init__(self, comm, pos, w, dst):
        self.comm, self.pos, self.w, self.dst = comm, pos, w, dst
        self.b = comm.take(GROUP)
        self.slot = lax.rem(pos.x, 2) * 2 + pos.c

    def each(self):
        for d in (1, 3, 2, 0):
            x = step4(self.pos.x, d)
            yield d, 0, x, self.w.at[:, pl.ds(0, F2_COLS)], pl.ds(0, F2_COLS)
            yield d, 1, x, self.w.at[:, pl.ds(pl.multiple_of((5 + x) * LANE, LANE), LANE)], pl.ds(F2_COLS, LANE)

    def ends(self, i, at):
        return self.dst.at[self.slot, :, at], self.comm.rsem.at[self.b + self.slot * 2 + i]

    def far(self, d, i, x, src, at):
        dst, r = self.ends(i, at)
        return pltpu.make_async_remote_copy(src_ref=src, dst_ref=dst, send_sem=self.comm.ssem.at[self.b + d * 2 + i], recv_sem=r,
                                            device_id=self.pos.dev(x=x, c=self.pos.x // 2), device_id_type=MESH)

    def near(self, d, i, x, src, at):
        return pltpu.make_async_copy(src, *self.ends(i, at))

    def start(self):
        mine = self.pos.c == self.pos.x // 2
        for v in self.each():
            if v[0]:
                self.far(*v).start()
            else:
                pl.when(jnp.logical_not(mine))(lambda v=v: self.far(*v).start())
                pl.when(mine)(lambda v=v: self.near(*v).start())

    def wait(self):
        for d, i, x, src, at in self.each():
            pltpu.make_async_copy(src, self.dst.at[d, :, at], self.comm.rsem.at[self.b + d * 2 + i]).wait()

    def drain(self):
        mine = self.pos.c == self.pos.x // 2
        for v in self.each():
            if v[0]:
                self.far(*v).wait_send()
            else:
                pl.when(jnp.logical_not(mine))(lambda v=v: self.far(*v).wait_send())


def pack_pieces(l, k, w_qkv, w_proj, w_fc1):
    def pieces(x, c, _):
        out, to = [], 0
        for o, n, step in slices(l, k):
            o += c * (N_A // 2)
            w = w_fc1 if k else w_qkv
            if k == 0 and o >= 3 * HIDDEN:
                w, o = w_proj, o - 3 * HIDDEN
            out.append((w.at[l, :, pl.ds(pl.multiple_of(o + x * step, LANE), n)], pl.ds(to, n)))
            to += n
        return out
    return pieces


def mod_pieces(l, w_ada):
    def pieces(x, c, _):
        return [(w_ada.at[l, :, pl.ds(pl.multiple_of(jnp.minimum(7 * (2 * x + c), 47) * LANE, LANE), W_MOD)], pl.ds(0, W_MOD))]
    return pieces


def rows72(recv, wide, packed, n):
    for p in range(GROUP):
        wide[9 * p:9 * p + 9, :n] = recv[p].astype(jnp.float32)
    packed[:, :n] = wide[:, :n].astype(jnp.bfloat16)


def slices(l, k):
    o, out = 0, []
    for a, b, c in SUBS[l, k]:
        out += [(o, (a + b) * LANE, 0), (o + (a + b) * LANE, c * LANE, c * LANE)]
        o += (a + b + RING * c) * LANE
    return out


def place_pack(pos, packed, g, l, k):
    base = pos.c * (N_A // 2)
    pairs, at = [], 0
    for o, n, step in slices(l, k):
        pairs.append((packed.at[:, pl.ds(at, n)], g.at[pos.z, rows_of(pos.y), pl.ds(pl.multiple_of(base + o + pos.x * step, LANE), n)]))
        at += n
    return pairs


class Modulation:
    def __init__(self, comm, pos, l, h, hv, s_all, b_ref, part, got, m, lsem):
        self.rings = mod_rings(comm, pos, h)
        self.l, self.hv, self.s_all, self.b, self.part, self.got, self.m = l, hv, s_all, b_ref, part, got, m
        self.load = pltpu.make_async_copy(h, hv, lsem)
        self.fan = Fan(comm, pos, lambda q: part.at[q], got)

    def ring(self, c, n):
        r = self.rings[c]
        if n % 2:
            r[n // 2].mid()
        else:
            if n:
                r[n // 2 - 1].end()
            if n < RING:
                r[n // 2].start()

    def drain(self):
        for c in self.rings:
            for q in c:
                q.drain()
        self.fan.drain()

    def stage(self, n):
        if n == 0:
            self.load.start()
        elif n == 1:
            self.load.wait()
            rows = self.s_all[...].reshape(64, HIDDEN).astype(jnp.bfloat16)
            w = self.hv[...].reshape(HIDDEN, W_MOD)
            v = jnp.dot(rows, w, preferred_element_type=jnp.float32) + self.b[self.l:self.l + 1, pl.ds(pl.multiple_of(jnp.minimum(7 * self.fan.p, 47) * LANE, LANE), W_MOD)].astype(jnp.float32)
            self.part[...] = v.astype(jnp.bfloat16).astype(jnp.float32).reshape(GROUP, GROUP, W_MOD)
            self.fan.start()
            self.got[self.fan.p] = self.part[self.fan.p]
        else:
            self.fan.wait()
            for q in range(7):
                self.m[self.l, :, W_MOD * q:W_MOD * (q + 1)] = self.got[q]
            self.m[self.l, :, 7 * W_MOD:6 * HIDDEN] = self.got[7][:, 2 * LANE:]


P, W, X, U, M, N, L, S = range(GROUP)
QKV, ATT, PROJ, FC1, FC2 = range(5)
STEPS = ((QKV, 6, 1.5, 0.8), (ATT, RING, 3.2, 0.0), (PROJ, RING, 1.3, 0.0), (FC1, 9, 1.8, 0.0), (FC2, RING, 3.9, 0.0))
LINK, ACROSS, HOP = 46.6e3, 600e3, 3.0
BLOCK = RUN * TILE


class Plan:
    def __init__(self):
        self.t, self.free, self.done, self.pend, self.slack = HOP, {}, set(), [], 0.0
        self.units = [(l, k, v) for l in range(NL) for k in range(3) for v in SUBS[l, k]]
        self.rank = [(3 * l + k, i) for i, (l, k, _) in enumerate(self.units)]
        self.landed, self.loaded, self.left = {}, {}, {}
        self.pre, self.slots = [], []
        for l in range(NL):
            for k in range(3):
                self.add(STARTS[3 * l + k], (P, l, k))
            self.add(STARTS[3 * NL + l], (P, l, 3))
        self.add(7.0, (S,))
        self.emit = self.pre
        for l in range(NL):
            self.until((N, l))
            self.t += 2.5
            for st, n, each, tail in STEPS:
                k = {QKV: 0, FC1: 1, FC2: 2}.get(st)
                if k is not None:
                    self.until((L, l, k))
                    self.t = max(self.t, self.loaded[l, k])
                for i in range(n):
                    self.t += each
                    if i == n - 1 and st >= PROJ:
                        self.done.add((L, l, st - PROJ, l))
                    self.emit = []
                    self.slack = 1.0
                    self.catch_up()
                    self.slots.append(((l, st, i), self.emit))
                self.t += tail

    def add(self, when, action):
        k = action[0]
        if k in (U, L):
            rank = self.rank[action[1]]
        elif k == S:
            rank = (0, -2)
        else:
            rank = (3 * action[1] + (action[2] if k in (P, W, X) and action[2] < 3 else 0), -1 if k == P and action[2] == 3 else 0)
        self.pend.append((when, rank, action))

    def due(self, p):
        return p[0] + (self.slack if p[2][0] in (U, M, W, X) else 0)

    def allowed(self, a):
        if a[0] == W and a[1]:
            return (X, a[1] - 1, a[2]) in self.done
        if a[0] == L and self.units[a[1]][0]:
            l, k, _ = self.units[a[1]]
            return (L, l - 1, k, l - 1) in self.done
        if a[0] == N and a[2] == 1:
            return (S,) in self.done
        if a[0] == N and a[2] == 0 and a[1]:
            return (N, a[1] - 1) in self.done
        return True

    def catch_up(self):
        while True:
            c = [p for p in self.pend if self.due(p) <= self.t and self.allowed(p[2])]
            if not c:
                return
            p = min(c, key=lambda v: (v[1], v[0]))
            self.pend.remove(p)
            self.emit.append(p[2])
            self.act(*p[2])

    def until(self, tag):
        self.slack = 0.0
        while True:
            self.catch_up()
            if tag in self.done:
                return
            self.t = max(self.t, min(p[0] for p in self.pend if self.allowed(p[2])))

    def both(self, link, size, rate=LINK):
        self.free[link] = max(self.t, self.free.get(link, self.t)) + size / rate
        return self.free[link] + HOP

    def ring(self, a, chain, size, n):
        if n == 2 * len(chain):
            return True
        big = size * RING ** (n // 2)
        self.add(self.both(chain[n // 2], big / 2 if n % 2 else big), a + (n + 1,))

    def act(self, kind, *n):
        if kind == P:
            l, k = n
            b = (W_F2, W_MOD)[k > 2] if k > 1 else width(l, k)
            self.add(self.both(0, 128 * b), (W, l, k))
        elif kind == W:
            self.t += 0.7
            self.add(self.t + 1.5, (X,) + n)
        elif kind == X:
            self.done.add((X,) + n)
            if n[1] == 3:
                for c in range(2):
                    self.add(self.t, (M, n[0], c, 0))
            for u, (l, k, _) in enumerate(self.units):
                if (l, k) == n:
                    for c in COLOURS:
                        self.add(self.t, (U, u, c, 0))
        elif kind == U:
            u, c, s = n
            l, k, v = self.units[u]
            size = v[c] * BLOCK * (2 if k == 2 else 1)
            chain = ((1, 2), (2, 1), (1, 2, 0))[c]
            if s == 2 * len(chain) + 1:
                self.landed[u] = self.landed.get(u, 0) + 1
                if self.landed[u] == 3:
                    self.add(self.t, (L, u))
            elif self.ring((U, u, c), chain, size, s):
                self.add(self.both(ACROSS, size * RING ** len(chain), ACROSS), (U, u, c, s + 1))
        elif kind == M:
            l, c, s = n
            if self.ring((M, l, c), ((2, 1), (1, 2))[c], (RING, 3)[c] * BLOCK, s):
                self.left[l] = self.left.get(l, 0) + 1
                if self.left[l] == 2:
                    self.add(self.t, (N, l, 0))
        elif kind == N:
            l, s = n
            if s == 2:
                self.done.add((N, l))
            else:
                self.t += 2.0 * s
                self.add(self.t + (4.5 if s else 2.5), (N, l, s + 1))
        elif kind == L:
            l, k, _ = self.units[n[0]]
            n_k = len(SUBS[l, k])
            self.loaded[l, k] = self.t + 1 + 3.5 / n_k
            self.left[L, l, k] = self.left.get((L, l, k), 0) + 1
            if self.left[L, l, k] == n_k:
                self.done.add((L, l, k))
        else:
            self.done.add((S,))


def step_kernel(x_ref, cond, w_ada, w_qkv, w_proj, w_fc1, w_fc2, ba, bq, bp, b1, b2, out, *refs):
    packs = (refs[0:RING], refs[RING:GROUP])
    u, x1, big, wq, wf, wg, rq0, rf0, rq1, rf1, rm, r2, wide, packed0, packed1, packed3, wide2, packed2, s_ref, s_all, hv, part, got, m, ssem, rsem, lsem, wsem = refs[GROUP:]
    plan = Plan()
    pos = Pos()
    comm = Comm(ssem, rsem)
    bufs = (wq, wf, wg)
    packed = (packed0, packed1, packed2, packed3)
    fan_s = Fan(comm, pos, lambda q: s_ref, s_all)
    fans, units, mods, loads, owner = [], [], [], [], []
    recvs = ((rq0, rf0, None, rm.at[0]), (rq1, rf1, None, rm.at[1]))
    for l in range(NL):
        gq, gf, g2, gm = packs[l]
        fans.append((Scatter(comm, pos, pack_pieces(l, 0, w_qkv, w_proj, w_fc1), recvs[l][0]), Scatter(comm, pos, pack_pieces(l, 1, w_qkv, w_proj, w_fc1), recvs[l][1]),
                     Scatter2(comm, pos, w_fc2.at[l], r2.at[l]), Scatter(comm, pos, mod_pieces(l, w_ada), recvs[l][3])))
        mods.append(Modulation(comm, pos, l, gm, hv, s_all, ba, part.at[l], got.at[l], m, lsem.at[10 + l]))
        for k in range(3):
            off, g, buf = 0, packs[l][k], bufs[k]
            for a, b, c in SUBS[l, k]:
                if k == 2:
                    units.append(Unit(comm, pos, fc2_unit(comm, pos, g, a * LANE)))
                    pairs = [(g, buf)]
                else:
                    units.append(Unit(comm, pos, pack_unit(comm, pos, g, off, a * LANE, b * LANE, c * LANE)))
                    n = (a + b + RING * c) * LANE
                    cols = [pl.ds(h * (N_A // 2) + off, n) for h in range(2)]
                    pairs = [(g.at[:, :, q], buf.at[:, :, q]) for q in cols]
                    off += n
                first = len(sum(loads, []))
                loads.append([pltpu.make_async_copy(s, d, wsem.at[first + i]) for i, (s, d) in enumerate(pairs)])
                owner.append((l, k))

    def ready(l, k):
        for own, cps in zip(owner, loads):
            if own == (l, k):
                for cp in cps:
                    cp.wait()

    def placing(l, i):
        g = packs[l][i]
        if i == 3:
            pairs = [(packed3.at[...], g.at[pos.z, rows_of(pos.y)])]
        elif i < 2:
            pairs = place_pack(pos, packed[i], g, l, i)
        else:
            full = pl.ds(pl.multiple_of(pos.c * HALF, GROUP), HALF)
            pairs = [(packed2.at[:, pl.ds(0, F2_COLS)], g.at[pos.z, pos.y, full, pl.ds(0, F2_COLS)]),
                     (packed2.at[:, pl.ds(F2_COLS, LANE)], g.at[pos.z, pos.y, full, pl.ds(pl.multiple_of((5 + pos.x) * LANE, LANE), LANE)])]
        return [pltpu.make_async_copy(a, b, lsem.at[(0, RING, 12, 14)[i] + k]) for k, (a, b) in enumerate(pairs)]

    def act(kind, *n):
        if kind == P:
            fans[n[0]][n[1]].start()
        elif kind == W:
            l, i = n
            fans[l][i].wait()
            if i == 2:
                for s in range(RING):
                    wide2[36 * s:36 * s + 36, :] = r2[l, s].astype(jnp.float32)
                packed2[...] = wide2[...].astype(jnp.bfloat16)
            else:
                rows72(recvs[l][i], wide, packed[i], W_MOD if i == 3 else width(l, i))
            for cp in placing(l, i):
                cp.start()
        elif kind == X:
            for cp in placing(*n):
                cp.wait()
        elif kind == U:
            units[n[0]].stage(n[1], n[2])
        elif kind == M:
            mods[n[0]].ring(n[1], n[2])
        elif kind == N:
            mods[n[0]].stage(n[1])
        elif kind == L:
            for cp in loads[n[0]]:
                cp.start()
        else:
            fan_s.wait()

    def ticker(l, stage):
        def tick(i):
            for (sl, ss, k), actions in plan.slots:
                if sl == l and ss == stage and actions:
                    @pl.when(i == k)
                    def _():
                        for v in actions:
                            act(*v)
        return tick

    s_ref[...] = jnp.zeros_like(s_ref)
    cv = cond[...].astype(jnp.float32)
    s_ref[0:RING, :] = jax.nn.silu(cv).astype(jnp.bfloat16).astype(jnp.float32)
    entry_barrier(pos)
    fan_s.start()
    s_all[fan_s.p] = s_ref[...]
    for v in plan.pre:
        act(*v)
    src = x_ref
    for l in range(NL):
        norm1(src, m, l, u)
        ready(l, 0)
        qkv_tiles(u, wq, bq, l, big, ticker(l, QKV))
        attend(big, u, ticker(l, ATT))
        proj_tiles(u, wq, bp, m, l, src, x1, u, ticker(l, PROJ))
        ready(l, 1)
        fc1_tiles(u, wf, b1, l, big, ticker(l, FC1))
        ready(l, 2)
        fc2_tiles(big, wg, b2, m, l, x1, out, ticker(l, FC2))
        src = out
    fan_s.drain()
    for l in range(NL):
        for f in fans[l]:
            f.drain()
        mods[l].drain()
    for v in units:
        v.drain()


N_SEM = GROUP + NL * (GROUP + GROUP + 16 + GROUP) + 16 * sum(len(v) for k, v in SUBS.items() if k[1] < 2) + 31 * sum(len(v) for v in SUBS.values())


def run_step(x, cond, w_ada, w_qkv, w_proj, w_fc1, w_fc2, ba, bq, bp, b1, b2):
    bf, f32 = jnp.bfloat16, jnp.float32
    shapes = [(RING, PLANE, N_A), (RING, PLANE, N_A), (RING, RING, PLANE, HIDDEN), (RING, PLANE, W_MOD)] * NL
    hbm = pl.BlockSpec(memory_space=pl.ANY)
    vm = pl.BlockSpec(memory_space=pltpu.VMEM)
    dma = pltpu.SemaphoreType.DMA
    return pl.pallas_call(
        step_kernel,
        out_shape=[jax.ShapeDtypeStruct((ROWS, HIDDEN), bf)] + [jax.ShapeDtypeStruct(s, bf) for s in shapes],
        in_specs=[vm, vm] + [hbm] * 5 + [vm] * 5, out_specs=[vm] + [hbm] * GROUP,
        scratch_shapes=[pltpu.VMEM((ROWS, HIDDEN), bf), pltpu.VMEM((ROWS, HIDDEN), bf), pltpu.VMEM((ROWS, N_A), bf),
                        pltpu.VMEM((RING, PLANE, N_A), bf), pltpu.VMEM((RING, PLANE, N_A), bf), pltpu.VMEM((RING, RING, PLANE, HIDDEN), bf),
                        *[pltpu.VMEM((GROUP, 9, width(l, k)), bf) for l in range(NL) for k in range(2)], pltpu.VMEM((NL, GROUP, 9, W_MOD), bf), pltpu.VMEM((NL, RING, 36, W_F2), bf),
                        pltpu.VMEM((RUN, 2048), f32), pltpu.VMEM((RUN, 2048), bf), pltpu.VMEM((RUN, 2048), bf), pltpu.VMEM((RUN, W_MOD), bf), pltpu.VMEM((HALF, W_F2), f32), pltpu.VMEM((HALF, W_F2), bf),
                        pltpu.VMEM((GROUP, HIDDEN), f32), pltpu.VMEM((GROUP, GROUP, HIDDEN), f32), pltpu.VMEM((RING, PLANE, W_MOD), bf), pltpu.VMEM((NL, GROUP, GROUP, W_MOD), f32), pltpu.VMEM((NL, GROUP, GROUP, W_MOD), f32),
                        pltpu.VMEM((NL, GROUP, 6 * HIDDEN), f32), dma((N_SEM,)), dma((N_SEM,)), dma((16,)), dma((2 * sum(len(v) for v in SUBS.values()),))],
        compiler_params=pltpu.CompilerParams(collective_id=0, has_side_effects=True, vmem_limit_bytes=67043328),
        name='dit_blocks',
    )(x, cond, w_ada, w_qkv, w_proj, w_fc1, w_fc2, ba, bq, bp, b1, b2)[0]


def solution(mesh):
    batch_spec = PartitionSpec(('dp', 'fsdp'), None, None)
    cond_spec = PartitionSpec(('dp', 'fsdp'), None)
    shard_spec = PartitionSpec(None, 'fsdp', None)
    bias_spec = PartitionSpec(None, None)

    def local_run(latents, cond_emb, w_ada, b_ada, w_qkv, b_qkv, w_proj, b_proj, w_fc1, b_fc1, w_fc2, b_fc2):
        y = run_step(latents.reshape(ROWS, HIDDEN), cond_emb, w_ada, w_qkv, w_proj, w_fc1, w_fc2, b_ada, b_qkv, b_proj, b_fc1, b_fc2)
        return y.reshape(latents.shape)

    in_specs = (batch_spec, cond_spec, shard_spec, bias_spec, shard_spec, bias_spec, shard_spec, bias_spec, shard_spec, bias_spec, shard_spec, bias_spec)
    return jax.shard_map(local_run, mesh=mesh, in_specs=in_specs, out_specs=batch_spec, check_vma=False)
```

time: 915 us -> 236 us (0.26); the launches traced: 905 us -> 235 us
  waiting for transfers between devices: 602 us -> 0 us
  Pallas kernels: 0 us -> 224 us
  matrix products: 209 us -> 0 us
  other arithmetic: 46.2 us -> 0 us
  local copies, waits for them, and re-layouts: 33.4 us -> 11.3 us
  between operations: 14.2 us -> 0.01 us
    all_gather x10 -> x0, waiting for transfers between devices: 598 us -> none  [gather_rows(): return lax.all_gather(shard, 'fsdp', axis=0, tiled=True)]
    pallas_call x0 -> x1, Pallas kernels: none -> 224 us  [run_step(): pl.pallas_call(step_kernel, out_shape=[jax.ShapeDtypeStruct((ROWS, HIDDEN...]
    dot_general x14 -> x0, matrix products: 209 us -> none  [the longest x2 51.9 us: value_a9(): jnp.einsum('toe,ef->tof', normed_b, full_fc1, preferred_element_type=jnp....]
    sub x2 -> x0, other arithmetic: 38.7 us -> none  [value_a9(): attn_probs = jax.nn.softmax(scores, axis=-1).astype(jnp.bfloat16)]
    convert_element_type x2 -> x0, local copies, waits for them, and re-layouts: 20.5 us -> none  [value_a9(): (jnp.einsum('toe,ef->tof', normed, full_qkv, preferred_element_type=jnp.f...]
    slice x5 -> x0, local copies, waits for them, and re-layouts: 9.93 us -> none  [the longest x1 2.42 us: local_run(): full_ada = gather_rows(w_ada[layer_idx])]
  transfers between devices with their start and end apart: 10 -> 0, of which waited for: 10 -> 0; matrix products, arithmetic and copies ran while one was open for 29% -> 0% of each run, Pallas kernels for 0% -> 0%
where the time goes in v1:
time: 236 us; the launch traced here: 235 us
  Pallas kernels  224 us (95%)
  local copies, waits for them, and re-layouts  11.3 us (5%)
    pallas_call x1, Pallas kernels, run_step(): pl.pallas_call(step_kernel, out_shape=[jax.ShapeDtypeStruct((ROWS, HIDDEN...  224 us
    unnamed x6, local copies, waits for them, and re-layouts  11.3 us

profile of v1, /device:TPU:1, one launch (start us, length us, event | category | flops | bytes accessed | tf_op | source)
XLA Modules:
  0.0 235.2 jit_solution(16005707724118686820)
XLA Ops:
  0.0 1.4 copy.15.w_proj
  1.4 1.6 copy.17.w_fc2
  3.0 1.6 copy.14.w_qkv
  4.6 1.7 copy.16.w_fc1
  6.3 1.8 copy.13.w_ada
  8.1 223.9 %dit_blocks.1 = (bf16[1024,1152]{1,0:T(8,128)(2,1)}, bf16[4,288,4608]{2,1,0:T(8,128)(2,1)}, bf16[4,288,4608]{2,1,0:T(8,128)(2,1)}, bf16[4,4,288,1152]{3,2,1,0:T(...) custom-call(bf16[1024,1152]{1,0:T(8,128)(2,1)} %bitcast.3, ...), custom_call_target="tpu_custom_call" | custom-call | tf_op jit(solution)/shard_map/dit_blocks/pallas_call | solution.py:812
  231.9 3.3 %copy.19 = bf16[4,256,1152]{2,1,0:T(8,128)(2,1)} copy(bf16[4,256,1152]{2,1,0:T(8,128)(2,1)} %bitcast.2) | data formatting | bytes 4718592

commit v2 on v1

--- a/solution.py
+++ b/solution.py
@@ -16,10 +16,9 @@
 N_A = 4608
 CUT_A = ((3, 2, 1), (2, 3, 1))
 CUT_B = ((2, 3, 1),)
-CUT_C = ((7, 7, 1),)
 CUT_D = ((3, 2, 1),)
-SUBS = {(l, k): cut for l, row in enumerate(((CUT_A, CUT_A, CUT_B), (CUT_A, CUT_C, CUT_D))) for k, cut in enumerate(row)}
-STARTS = (3, 17, 31, 47, 71, 99, 3, 58)
+SUBS = {(l, k): cut for l, row in enumerate(((CUT_A, CUT_A, CUT_B), (CUT_A, CUT_A, CUT_D))) for k, cut in enumerate(row)}
+STARTS = (3, 16, 33, 9, 62, 86, 117, 78)
 COLOURS = (1, 2, 0)
 
 
@@ -379,7 +378,7 @@
                     yield c, d, i, x, src, at
 
     def ends(self, d, i, at):
-        return self.dst.at[2 * self.pos.x + self.pos.c, :, at], self.comm.rsem.at[self.b + (self.pos.c * RING + d) * self.n + i]
+        return self.dst.at[2 * self.pos.x + self.pos.c, :, :, at], self.comm.rsem.at[self.b + (self.pos.c * RING + d) * self.n + i]
 
     def far(self, c, d, i, x, src, at):
         dst, r = self.ends(d, i, at)
@@ -399,7 +398,7 @@
 
     def wait(self):
         for c, d, i, x, src, at in self.each():
-            dst = self.dst.at[2 * step4(self.pos.x, -d) + c, :, at]
+            dst = self.dst.at[2 * step4(self.pos.x, -d) + c, :, :, at]
             pltpu.make_async_copy(src, dst, self.comm.rsem.at[self.b + (c * RING + d) * self.n + i]).wait()
 
     def drain(self):
@@ -419,11 +418,11 @@
     def each(self):
         for d in (1, 3, 2, 0):
             x = step4(self.pos.x, d)
-            yield d, 0, x, self.w.at[:, pl.ds(0, F2_COLS)], pl.ds(0, F2_COLS)
-            yield d, 1, x, self.w.at[:, pl.ds(pl.multiple_of((5 + x) * LANE, LANE), LANE)], pl.ds(F2_COLS, LANE)
+            yield d, 0, x, self.w.at[:, :, pl.ds(0, F2_COLS)], pl.ds(0, F2_COLS)
+            yield d, 1, x, self.w.at[:, :, pl.ds(pl.multiple_of((5 + x) * LANE, LANE), LANE)], pl.ds(F2_COLS, LANE)
 
     def ends(self, i, at):
-        return self.dst.at[self.slot, :, at], self.comm.rsem.at[self.b + self.slot * 2 + i]
+        return self.dst.at[self.slot, :, :, at], self.comm.rsem.at[self.b + self.slot * 2 + i]
 
     def far(self, d, i, x, src, at):
         dst, r = self.ends(i, at)
@@ -444,7 +443,7 @@
 
     def wait(self):
         for d, i, x, src, at in self.each():
-            pltpu.make_async_copy(src, self.dst.at[d, :, at], self.comm.rsem.at[self.b + d * 2 + i]).wait()
+            pltpu.make_async_copy(src, self.dst.at[d, :, :, at], self.comm.rsem.at[self.b + d * 2 + i]).wait()
 
     def drain(self):
         mine = self.pos.c == self.pos.x // 2
@@ -455,29 +454,34 @@
                 pl.when(jnp.logical_not(mine))(lambda v=v: self.far(*v).wait_send())
 
 
-def pack_pieces(l, k, w_qkv, w_proj, w_fc1):
+def pack_pieces(k, w_qkv, w_proj, w_fc1):
     def pieces(x, c, _):
         out, to = [], 0
-        for o, n, step in slices(l, k):
+        for o, n, step in slices(0, k):
             o += c * (N_A // 2)
             w = w_fc1 if k else w_qkv
             if k == 0 and o >= 3 * HIDDEN:
                 w, o = w_proj, o - 3 * HIDDEN
-            out.append((w.at[l, :, pl.ds(pl.multiple_of(o + x * step, LANE), n)], pl.ds(to, n)))
+            out.append((w.at[:, :, pl.ds(pl.multiple_of(o + x * step, LANE), n)], pl.ds(to, n)))
             to += n
         return out
     return pieces
 
 
-def mod_pieces(l, w_ada):
+def mod_pieces(w_ada):
     def pieces(x, c, _):
-        return [(w_ada.at[l, :, pl.ds(pl.multiple_of(jnp.minimum(7 * (2 * x + c), 47) * LANE, LANE), W_MOD)], pl.ds(0, W_MOD))]
+        return [(w_ada.at[:, :, pl.ds(pl.multiple_of(jnp.minimum(7 * (2 * x + c), 47) * LANE, LANE), W_MOD)], pl.ds(0, W_MOD))]
     return pieces
 
 
-def rows72(recv, wide, packed, n):
-    for p in range(GROUP):
-        wide[9 * p:9 * p + 9, :n] = recv[p].astype(jnp.float32)
+def lay_rows(recv, l, wide, packed, n):
+    devs, rows = recv.shape[0], recv.shape[1]
+
+    def body(p, _):
+        for r in range(rows):
+            wide[pl.ds(p * rows + r, 1), :n] = recv[p, r].astype(jnp.float32)[l:l + 1, :]
+        return 0
+    lax.fori_loop(0, devs, body, 0)
     packed[:, :n] = wide[:, :n].astype(jnp.bfloat16)
 
 
@@ -553,10 +557,8 @@
         self.rank = [(3 * l + k, i) for i, (l, k, _) in enumerate(self.units)]
         self.landed, self.loaded, self.left = {}, {}, {}
         self.pre, self.slots = [], []
-        for l in range(NL):
-            for k in range(3):
-                self.add(STARTS[3 * l + k], (P, l, k))
-            self.add(STARTS[3 * NL + l], (P, l, 3))
+        for k in range(RING):
+            self.add(STARTS[k], (P, k))
         self.add(7.0, (S,))
         self.emit = self.pre
         for l in range(NL):
@@ -584,15 +586,13 @@
         elif k == S:
             rank = (0, -2)
         else:
-            rank = (3 * action[1] + (action[2] if k in (P, W, X) and action[2] < 3 else 0), -1 if k == P and action[2] == 3 else 0)
+            rank = (3 * action[1], 0) if k in (M, N) else (action[1] % 3, -action[1] // 3)
         self.pend.append((when, rank, action))
 
     def due(self, p):
         return p[0] + (self.slack if p[2][0] in (U, M, W, X) else 0)
 
     def allowed(self, a):
-        if a[0] == W and a[1]:
-            return (X, a[1] - 1, a[2]) in self.done
         if a[0] == L and self.units[a[1]][0]:
             l, k, _ = self.units[a[1]]
             return (L, l - 1, k, l - 1) in self.done
@@ -632,21 +632,23 @@
 
     def act(self, kind, *n):
         if kind == P:
-            l, k = n
-            b = (W_F2, W_MOD)[k > 2] if k > 1 else width(l, k)
-            self.add(self.both(0, 128 * b), (W, l, k))
+            k, = n
+            b = (W_F2, W_MOD)[k > 2] if k > 1 else width(0, k)
+            self.add(self.both(0, HALF * b), (W, k))
         elif kind == W:
-            self.t += 0.7
+            self.t += 1.5
             self.add(self.t + 1.5, (X,) + n)
         elif kind == X:
-            self.done.add((X,) + n)
-            if n[1] == 3:
-                for c in range(2):
-                    self.add(self.t, (M, n[0], c, 0))
-            for u, (l, k, _) in enumerate(self.units):
-                if (l, k) == n:
-                    for c in COLOURS:
-                        self.add(self.t, (U, u, c, 0))
+            k, = n
+            for l in range(NL):
+                at = max(self.t, STARTS[RING + k] * l)
+                if k == 3:
+                    for c in range(2):
+                        self.add(at, (M, l, c, 0))
+                for u, own in enumerate(self.units):
+                    if own[:2] == (l, k):
+                        for c in COLOURS:
+                            self.add(at, (U, u, c, 0))
         elif kind == U:
             u, c, s = n
             l, k, v = self.units[u]
@@ -684,20 +686,20 @@
 
 def step_kernel(x_ref, cond, w_ada, w_qkv, w_proj, w_fc1, w_fc2, ba, bq, bp, b1, b2, out, *refs):
     packs = (refs[0:RING], refs[RING:GROUP])
-    u, x1, big, wq, wf, wg, rq0, rf0, rq1, rf1, rm, r2, wide, packed0, packed1, packed3, wide2, packed2, s_ref, s_all, hv, part, got, m, ssem, rsem, lsem, wsem = refs[GROUP:]
+    u, x1, big, wq, wf, wg, rq, rf, r2, rm, wide, wide2, s_ref, s_all, hv, part, got, m, ssem, rsem, lsem, wsem = refs[GROUP:-GROUP]
+    packed = (refs[-GROUP:-RING], refs[-RING:])
     plan = Plan()
     pos = Pos()
     comm = Comm(ssem, rsem)
     bufs = (wq, wf, wg)
-    packed = (packed0, packed1, packed2, packed3)
     fan_s = Fan(comm, pos, lambda q: s_ref, s_all)
-    fans, units, mods, loads, owner = [], [], [], [], []
-    recvs = ((rq0, rf0, None, rm.at[0]), (rq1, rf1, None, rm.at[1]))
+    units, mods, loads, owner = [], [], [], []
+    recvs = (rq, rf, r2, rm)
+    fans = (Scatter(comm, pos, pack_pieces(0, w_qkv, w_proj, w_fc1), rq), Scatter(comm, pos, pack_pieces(1, w_qkv, w_proj, w_fc1), rf),
+            Scatter2(comm, pos, w_fc2, r2), Scatter(comm, pos, mod_pieces(w_ada), rm))
     for l in range(NL):
         gq, gf, g2, gm = packs[l]
-        fans.append((Scatter(comm, pos, pack_pieces(l, 0, w_qkv, w_proj, w_fc1), recvs[l][0]), Scatter(comm, pos, pack_pieces(l, 1, w_qkv, w_proj, w_fc1), recvs[l][1]),
-                     Scatter2(comm, pos, w_fc2.at[l], r2.at[l]), Scatter(comm, pos, mod_pieces(l, w_ada), recvs[l][3])))
-        mods.append(Modulation(comm, pos, l, gm, hv, s_all, ba, part.at[l], got.at[l], m, lsem.at[10 + l]))
+        mods.append(Modulation(comm, pos, l, gm, hv, s_all, ba, part.at[l], got.at[l], m, lsem.at[RING * GROUP + l]))
         for k in range(3):
             off, g, buf = 0, packs[l][k], bufs[k]
             for a, b, c in SUBS[l, k]:
@@ -720,31 +722,29 @@
                 for cp in cps:
                     cp.wait()
 
-    def placing(l, i):
-        g = packs[l][i]
-        if i == 3:
-            pairs = [(packed3.at[...], g.at[pos.z, rows_of(pos.y)])]
-        elif i < 2:
-            pairs = place_pack(pos, packed[i], g, l, i)
-        else:
-            full = pl.ds(pl.multiple_of(pos.c * HALF, GROUP), HALF)
-            pairs = [(packed2.at[:, pl.ds(0, F2_COLS)], g.at[pos.z, pos.y, full, pl.ds(0, F2_COLS)]),
-                     (packed2.at[:, pl.ds(F2_COLS, LANE)], g.at[pos.z, pos.y, full, pl.ds(pl.multiple_of((5 + pos.x) * LANE, LANE), LANE)])]
-        return [pltpu.make_async_copy(a, b, lsem.at[(0, RING, 12, 14)[i] + k]) for k, (a, b) in enumerate(pairs)]
+    def placing(i):
+        pairs = []
+        for l in range(NL):
+            g, block = packs[l][i], packed[l][i]
+            if i == 3:
+                pairs.append((block, g.at[pos.z, rows_of(pos.y)]))
+            elif i < 2:
+                pairs += place_pack(pos, block, g, l, i)
+            else:
+                full = pl.ds(pl.multiple_of(pos.c * HALF, GROUP), HALF)
+                pairs += [(block.at[:, pl.ds(0, F2_COLS)], g.at[pos.z, pos.y, full, pl.ds(0, F2_COLS)]),
+                          (block.at[:, pl.ds(F2_COLS, LANE)], g.at[pos.z, pos.y, full, pl.ds(pl.multiple_of(F2_COLS + pos.x * LANE, LANE), LANE)])]
+        return [pltpu.make_async_copy(a, b, lsem.at[i * GROUP + k]) for k, (a, b) in enumerate(pairs)]
 
     def act(kind, *n):
         if kind == P:
-            fans[n[0]][n[1]].start()
+            fans[n[0]].start()
         elif kind == W:
-            l, i = n
-            fans[l][i].wait()
-            if i == 2:
-                for s in range(RING):
-                    wide2[36 * s:36 * s + 36, :] = r2[l, s].astype(jnp.float32)
-                packed2[...] = wide2[...].astype(jnp.bfloat16)
-            else:
-                rows72(recvs[l][i], wide, packed[i], W_MOD if i == 3 else width(l, i))
-            for cp in placing(l, i):
+            i, = n
+            fans[i].wait()
+            for l in range(NL):
+                lay_rows(recvs[i], l, wide2 if i == 2 else wide, packed[l][i], recvs[i].shape[-1])
+            for cp in placing(i):
                 cp.start()
         elif kind == X:
             for cp in placing(*n):
@@ -792,15 +792,15 @@
         fc2_tiles(big, wg, b2, m, l, x1, out, ticker(l, FC2))
         src = out
     fan_s.drain()
-    for l in range(NL):
-        for f in fans[l]:
-            f.drain()
-        mods[l].drain()
+    for v in fans:
+        v.drain()
+    for v in mods:
+        v.drain()
     for v in units:
         v.drain()
 
 
-N_SEM = GROUP + NL * (GROUP + GROUP + 16 + GROUP) + 16 * sum(len(v) for k, v in SUBS.items() if k[1] < 2) + 31 * sum(len(v) for v in SUBS.values())
+N_SEM = GROUP * (3 + RING * NL) + 16 * sum(len(SUBS[0, k]) for k in range(2)) + 31 * sum(len(v) for v in SUBS.values()) + 8 * GROUP
 
 
 def run_step(x, cond, w_ada, w_qkv, w_proj, w_fc1, w_fc2, ba, bq, bp, b1, b2):
@@ -809,16 +809,19 @@
     hbm = pl.BlockSpec(memory_space=pl.ANY)
     vm = pl.BlockSpec(memory_space=pltpu.VMEM)
     dma = pltpu.SemaphoreType.DMA
+    wide = [width(0, k) for k in range(2)]
     return pl.pallas_call(
         step_kernel,
         out_shape=[jax.ShapeDtypeStruct((ROWS, HIDDEN), bf)] + [jax.ShapeDtypeStruct(s, bf) for s in shapes],
         in_specs=[vm, vm] + [hbm] * 5 + [vm] * 5, out_specs=[vm] + [hbm] * GROUP,
         scratch_shapes=[pltpu.VMEM((ROWS, HIDDEN), bf), pltpu.VMEM((ROWS, HIDDEN), bf), pltpu.VMEM((ROWS, N_A), bf),
                         pltpu.VMEM((RING, PLANE, N_A), bf), pltpu.VMEM((RING, PLANE, N_A), bf), pltpu.VMEM((RING, RING, PLANE, HIDDEN), bf),
-                        *[pltpu.VMEM((GROUP, 9, width(l, k)), bf) for l in range(NL) for k in range(2)], pltpu.VMEM((NL, GROUP, 9, W_MOD), bf), pltpu.VMEM((NL, RING, 36, W_F2), bf),
-                        pltpu.VMEM((RUN, 2048), f32), pltpu.VMEM((RUN, 2048), bf), pltpu.VMEM((RUN, 2048), bf), pltpu.VMEM((RUN, W_MOD), bf), pltpu.VMEM((HALF, W_F2), f32), pltpu.VMEM((HALF, W_F2), bf),
-                        pltpu.VMEM((GROUP, HIDDEN), f32), pltpu.VMEM((GROUP, GROUP, HIDDEN), f32), pltpu.VMEM((RING, PLANE, W_MOD), bf), pltpu.VMEM((NL, GROUP, GROUP, W_MOD), f32), pltpu.VMEM((NL, GROUP, GROUP, W_MOD), f32),
-                        pltpu.VMEM((NL, GROUP, 6 * HIDDEN), f32), dma((N_SEM,)), dma((N_SEM,)), dma((16,)), dma((2 * sum(len(v) for v in SUBS.values()),))],
+                        pltpu.VMEM((GROUP, 9, NL, wide[0]), bf), pltpu.VMEM((GROUP, 9, NL, wide[1]), bf), pltpu.VMEM((RING, 36, NL, W_F2), bf), pltpu.VMEM((GROUP, 9, NL, W_MOD), bf),
+                        pltpu.VMEM((RUN, max(wide)), f32), pltpu.VMEM((HALF, W_F2), f32),
+                        pltpu.VMEM((GROUP, HIDDEN), f32), pltpu.VMEM((GROUP, GROUP, HIDDEN), f32), pltpu.VMEM((RING, PLANE, W_MOD), bf),
+                        pltpu.VMEM((NL, GROUP, GROUP, W_MOD), f32), pltpu.VMEM((NL, GROUP, GROUP, W_MOD), f32), pltpu.VMEM((NL, GROUP, 6 * HIDDEN), f32),
+                        dma((N_SEM,)), dma((N_SEM,)), dma((5 * GROUP,)), dma((2 * sum(len(v) for v in SUBS.values()),))]
+        + [pltpu.VMEM((n, c), bf) for _ in range(NL) for n, c in ((RUN, wide[0]), (RUN, wide[1]), (HALF, W_F2), (RUN, W_MOD))],
         compiler_params=pltpu.CompilerParams(collective_id=0, has_side_effects=True, vmem_limit_bytes=67043328),
         name='dit_blocks',
     )(x, cond, w_ada, w_qkv, w_proj, w_fc1, w_fc2, ba, bq, bp, b1, b2)[0]
@@ -831,7 +834,7 @@
     bias_spec = PartitionSpec(None, None)
 
     def local_run(latents, cond_emb, w_ada, b_ada, w_qkv, b_qkv, w_proj, b_proj, w_fc1, b_fc1, w_fc2, b_fc2):
-        y = run_step(latents.reshape(ROWS, HIDDEN), cond_emb, w_ada, w_qkv, w_proj, w_fc1, w_fc2, b_ada, b_qkv, b_proj, b_fc1, b_fc2)
+        y = run_step(latents.reshape(ROWS, HIDDEN), cond_emb, *[jnp.swapaxes(w, 0, 1) for w in (w_ada, w_qkv, w_proj, w_fc1, w_fc2)], b_ada, b_qkv, b_proj, b_fc1, b_fc2)
         return y.reshape(latents.shape)
 
     in_specs = (batch_spec, cond_spec, shard_spec, bias_spec, shard_spec, bias_spec, shard_spec, bias_spec, shard_spec, bias_spec, shard_spec, bias_spec)

time: 236 us -> 233 us (0.987)
  local copies, waits for them, and re-layouts: 11.3 us -> 3.25 us
  Pallas kernels: 224 us -> 229 us
    unnamed x6 -> x1, local copies, waits for them, and re-layouts: 11.3 us -> 3.25 us
    pallas_call x1, Pallas kernels: 224 us -> 229 us  [run_step(): pl.pallas_call(step_kernel, out_shape=[jax.ShapeDtypeStruct((ROWS, HIDDEN...]
where the time goes in v2:
time: 233 us; the launch traced here: 232 us
  Pallas kernels  229 us (98%)
  local copies, waits for them, and re-layouts  3.25 us (1%)
    pallas_call x1, Pallas kernels, run_step(): pl.pallas_call(step_kernel, out_shape=[jax.ShapeDtypeStruct((ROWS, HIDDEN...  229 us

profile of v2, /device:TPU:1, one launch (start us, length us, event | category | flops | bytes accessed | tf_op | source)
XLA Modules:
  0.0 231.9 jit_solution(7404745166849373577)
XLA Ops:
  0.0 228.7 %dit_blocks.1 = (bf16[1024,1152]{1,0:T(8,128)(2,1)}, bf16[4,288,4608]{2,1,0:T(8,128)(2,1)}, bf16[4,288,4608]{2,1,0:T(8,128)(2,1)}, bf16[4,4,288,1152]{3,2,1,0:T(...) custom-call(bf16[1024,1152]{1,0:T(8,128)(2,1)} %bitcast.7, ...), custom_call_target="tpu_custom_call" | custom-call | tf_op jit(solution)/shard_map/dit_blocks/pallas_call | solution.py:813
  228.7 3.3 %copy.14 = bf16[4,256,1152]{2,1,0:T(8,128)(2,1)} copy(bf16[4,256,1152]{2,1,0:T(8,128)(2,1)} %bitcast.8) | data formatting | bytes 4718592

commit v3 on v2

--- a/solution.py
+++ b/solution.py
@@ -18,7 +18,7 @@
 CUT_B = ((2, 3, 1),)
 CUT_D = ((3, 2, 1),)
 SUBS = {(l, k): cut for l, row in enumerate(((CUT_A, CUT_A, CUT_B), (CUT_A, CUT_A, CUT_D))) for k, cut in enumerate(row)}
-STARTS = (3, 16, 33, 9, 62, 86, 117, 78)
+STARTS = (3, 19, 35, 3, 64, 85, 117, 83)
 COLOURS = (1, 2, 0)
 
 
@@ -66,40 +66,41 @@
 class Ring:
     def __init__(self, comm, pos, axis, sel, half):
         self.comm, self.sel, self.half = comm, sel, half
-        self.b = comm.take(RING)
+        self.b = comm.take(6)
         me = getattr(pos, axis)
         self.me, self.r, self.l, self.o = me, step4(me, 1), step4(me, -1), step4(me, 2)
         self.right, self.left = pos.dev(**{axis: self.r}), pos.dev(**{axis: self.l})
 
+    def hop(self, i, chip, h):
+        ref = self.half(chip, h)
+        return self.comm.copy(ref, ref, self.b + i, self.left if i % 2 else self.right)
+
+    def sent(self):
+        return [self.hop(i, self.me, h) for i, h in enumerate((0, 1, 1, 0))]
+
+    def passed(self):
+        return self.hop(RING, self.l, 0), self.hop(5, self.r, 1)
+
     def start(self):
-        own = self.sel(self.me)
-        self.comm.copy(own, own, self.b, self.right).start()
-        self.comm.copy(own, own, self.b + 1, self.left).start()
+        for m in self.sent():
+            m.start()
 
     def mid(self):
-        a = self.sel(self.l)
-        self.comm.copy(a, a, self.b, self.right).wait_recv()
-        h = self.half(self.l, 0)
-        self.comm.copy(h, h, self.b + 2, self.right).start()
-        a = self.sel(self.r)
-        self.comm.copy(a, a, self.b + 1, self.left).wait_recv()
-        h = self.half(self.r, 1)
-        self.comm.copy(h, h, self.b + 3, self.left).start()
+        for i, m in enumerate(self.passed()):
+            self.hop(i, (self.l, self.r)[i], i).wait_recv()
+            m.start()
 
     def end(self):
-        h = self.half(self.o, 0)
-        self.comm.copy(h, h, self.b + 2, self.right).wait_recv()
-        h = self.half(self.o, 1)
-        self.comm.copy(h, h, self.b + 3, self.left).wait_recv()
+        self.hop(2, self.l, 1).wait_recv()
+        self.hop(3, self.r, 0).wait_recv()
+        self.hop(RING, self.o, 0).wait_recv()
+        self.hop(5, self.o, 1).wait_recv()
 
     def drain(self):
-        own = self.sel(self.me)
-        self.comm.copy(own, own, self.b, self.right).wait_send()
-        self.comm.copy(own, own, self.b + 1, self.left).wait_send()
-        h = self.half(self.l, 0)
-        self.comm.copy(h, h, self.b + 2, self.right).wait_send()
-        h = self.half(self.r, 1)
-        self.comm.copy(h, h, self.b + 3, self.left).wait_send()
+        for m in self.sent():
+            m.wait_send()
+        for m in self.passed():
+            m.wait_send()
 
 
 def pack_unit(comm, pos, g, off, wa, wb, wc):
@@ -546,7 +547,7 @@
 P, W, X, U, M, N, L, S = range(GROUP)
 QKV, ATT, PROJ, FC1, FC2 = range(5)
 STEPS = ((QKV, 6, 1.5, 0.8), (ATT, RING, 3.2, 0.0), (PROJ, RING, 1.3, 0.0), (FC1, 9, 1.8, 0.0), (FC2, RING, 3.9, 0.0))
-LINK, ACROSS, HOP = 46.6e3, 600e3, 3.0
+LINK, ACROSS, HOP = 46.6e3, 600e3, 3.8
 BLOCK = RUN * TILE
 
 
@@ -627,8 +628,10 @@
     def ring(self, a, chain, size, n):
         if n == 2 * len(chain):
             return True
-        big = size * RING ** (n // 2)
-        self.add(self.both(chain[n // 2], big / 2 if n % 2 else big), a + (n + 1,))
+        half = size * RING ** (n // 2) / 2
+        self.add(self.both(chain[n // 2], half), a + (n + 1,))
+        if n % 2 == 0:
+            self.both(chain[n // 2], half)
 
     def act(self, kind, *n):
         if kind == P:
@@ -800,7 +803,7 @@
         v.drain()
 
 
-N_SEM = GROUP * (3 + RING * NL) + 16 * sum(len(SUBS[0, k]) for k in range(2)) + 31 * sum(len(v) for v in SUBS.values()) + 8 * GROUP
+N_SEM = GROUP * (3 + RING * NL) + 16 * sum(len(SUBS[0, k]) for k in range(2)) + 45 * sum(len(v) for v in SUBS.values()) + 8 * GROUP
 
 
 def run_step(x, cond, w_ada, w_qkv, w_proj, w_fc1, w_fc2, ba, bq, bp, b1, b2):

time: 233 us -> 227 us (0.974)
  Pallas kernels: 229 us -> 224 us
    pallas_call x1, Pallas kernels: 229 us -> 224 us  [run_step(): pl.pallas_call(step_kernel, out_shape=[jax.ShapeDtypeStruct((ROWS, HIDDEN...]
where the time goes in v3:
time: 227 us
  Pallas kernels  224 us (99%)
  local copies, waits for them, and re-layouts  3.25 us (1%)
    pallas_call x1, Pallas kernels, run_step(): pl.pallas_call(step_kernel, out_shape=[jax.ShapeDtypeStruct((ROWS, HIDDEN...  224 us

profile of v3, /device:TPU:1, one launch (start us, length us, event | category | flops | bytes accessed | tf_op | source)
XLA Modules:
  0.0 227.1 jit_solution(12441700276821104467)
XLA Ops:
  0.0 223.8 %dit_blocks.1 = (bf16[1024,1152]{1,0:T(8,128)(2,1)}, bf16[4,288,4608]{2,1,0:T(8,128)(2,1)}, bf16[4,288,4608]{2,1,0:T(8,128)(2,1)}, bf16[4,4,288,1152]{3,2,1,0:T(...) custom-call(bf16[1024,1152]{1,0:T(8,128)(2,1)} %bitcast.7, ...), custom_call_target="tpu_custom_call" | custom-call | tf_op jit(solution)/shard_map/dit_blocks/pallas_call | solution.py:816
  223.8 3.3 %copy.14 = bf16[4,256,1152]{2,1,0:T(8,128)(2,1)} copy(bf16[4,256,1152]{2,1,0:T(8,128)(2,1)} %bitcast.8) | data formatting | bytes 4718592
